TPU v7x, 256 devices: a whole 4x4x8 slice. The times are simulated.
256 devices in a mesh: rep: 8 (over z_lo, y), shard: 32 (over z_hi, x, core).
Axes of the slice: x: 4, y: 4, z: 8 (z_hi: 4, z_lo: 2; z = z_hi * 2 + z_lo), core: 2. Of those that a mesh axis runs over, the one named last changes fastest.
Arguments:
- activations: bfloat16 [262144, 2048], P(('rep', 'shard')), may hold values from -24 to 24
- cotangents: bfloat16 [262144, 1024], P(('rep', 'shard')), may hold values from -1024 to 1024
- inner_params: float32 [8, 2048, 1024], P('rep', 'shard'), may hold values from -6 to 6
- inner_moment: float32 [8, 2048, 1024], P('rep', 'shard'), may hold values from 0.25 to 4
- outer_params: float32 [2048, 1024], P('shard'), may hold values from -6 to 6
- momentum: float32 [2048, 1024], P('shard'), may hold values from -3 to 3
Outputs:
- new_params: float32 [2048, 1024], P('shard')
- new_momentum: float32 [2048, 1024], P('shard')
- compute_copy: bfloat16 [2048, 1024], replicated
All inputs are finite; a program needn't handle non-finite values.
Results may differ from a plain program's by a relative error of at most 0.007.
Values may be sent and summed in bfloat16 or wider, within the bound.
A program may use at most 64 MiB of HBM per device.

v0:
```python
import jax
import jax.numpy as jnp
from jax import lax
from jax.sharding import Mesh
from jax.sharding import PartitionSpec as P

SHARD = ("shard_0", "shard_1", "shard_2")
REP_SHARD = ("rep", "shard_0", "shard_1", "shard_2")


outer_rate = 0.7
inertia = 0.9
inner_rate = 0.3
epsilon = 1e-08


def cut_along(array, dim, length):
    before, after = (array.shape[:dim], array.shape[dim + 1 :])
    return jnp.moveaxis(array.reshape(*before, length, -1, *after), dim, 0)


def sum_at_owner(array, axis, dim):
    length = lax.axis_size(axis)
    blocks = lax.all_to_all(cut_along(array, dim, length), axis, 0, 0, tiled=True)
    return jnp.sum(blocks.astype(jnp.float32), axis=0)


def summed_rows(array, axes, dim):
    far, near = axes
    own = sum_at_owner(cut_along(array, dim, lax.axis_size(far)), near, dim + 1)
    return jnp.sum(
        lax.all_to_all(own.astype(jnp.bfloat16), far, 0, 0, tiled=True).astype(jnp.float32), axis=0
    )


def copy_for_each(array, axis):
    length = lax.axis_size(axis)
    return lax.all_to_all(
        jnp.broadcast_to(array[None], (length, *array.shape)), axis, 0, 0, tiled=True
    )


def taken_together(array, axis):
    return copy_for_each(array, axis).sum(axis=0)


def joined_along(blocks, dim):
    blocks = jnp.moveaxis(blocks, 0, dim)
    dims = blocks.shape
    return blocks.reshape(*dims[:dim], dims[dim] * dims[dim + 1], *dims[dim + 2 :])


def gather_axes(array, axes, dim):
    far, near = axes
    blocks = copy_for_each(copy_for_each(array, far), near)
    return joined_along(blocks.swapaxes(0, 1).reshape(-1, *array.shape), dim)


def outer_step(pseudo_grad, outer_rows, moment_rows):
    fresh_moment = inertia * moment_rows + pseudo_grad
    fresh_params = outer_rows - outer_rate * (pseudo_grad + inertia * fresh_moment)
    return (fresh_params, fresh_moment)


def per_device(activations, cotangents, inner_params, inner_moment, outer_params, momentum):
    shard_count = lax.axis_size(SHARD)
    group_count = lax.axis_size("rep")
    group_tok = activations.shape[0] * shard_count
    summed = summed_rows(
        lax.dot_general(
            activations, cotangents, (((0,), (0,)), ((), ())), preferred_element_type=jnp.float32
        ).astype(jnp.bfloat16),
        (("shard_0", "shard_1"), "shard_2"),
        0,
    )
    mean_grad = summed / group_tok
    replica_params = inner_params[0] - inner_rate * mean_grad / (
        jnp.sqrt(inner_moment[0]) + epsilon
    )
    param_delta = outer_params - replica_params
    pseudo_grad = taken_together(param_delta, "rep") / group_count
    new_params, new_momentum = outer_step(pseudo_grad, outer_params, momentum)
    compute_copy = gather_axes(
        new_params.astype(jnp.bfloat16), (("shard_0", "shard_1"), "shard_2"), 0
    )
    return (new_params, new_momentum, compute_copy)


def solution(mesh):
    split = Mesh(
        mesh.devices.reshape(mesh.shape["rep"], 4, 4, 2), ("rep", "shard_0", "shard_1", "shard_2")
    )
    return jax.shard_map(
        per_device,
        mesh=split,
        in_specs=(
            P(REP_SHARD, None),
            P(REP_SHARD, None),
            P("rep", SHARD, None),
            P("rep", SHARD, None),
            P(SHARD, None),
            P(SHARD, None),
        ),
        out_specs=(P(SHARD, None), P(SHARD, None), P()),
        check_vma=False,
    )
```

profile of v0, /device:TPU:1, one launch (start us, length us, event | category | flops | bytes accessed | tf_op | source)
XLA Modules:
  0.0 186.3 jit_solution(12103849303355610141)
XLA Ops:
  0.6 0.0 copy-start
  0.6 1.6 copy-done
  2.2 7.0 %convolution_convert_fusion = bf16[2048,1024]{1,0:T(8,128)(2,1)S(1)} fusion(bf16[1024,2048]{1,0:T(8,128)(2,1)} %param.6, bf16[1024,1024]{1,0:T(8,128)(2,1)S(1)} %copy-done), kind=kOutput, calls=%fused_computation.2 | convolution fusion | flops 4297064448 | bytes 10485760 | tf_op jit(solution)/shard_map/dot_general | solution.py:70
  9.2 0.7 copy.15
  9.9 11.0 %all_to_all.25 = bf16[2,16,64,1024]{3,2,1,0:T(8,128)(2,1)} all-to-all(bf16[2,16,64,1024]{3,2,1,0:T(8,128)(2,1)S(1)} %bitcast.17), channel_id=1, replica_groups=mesh['rep'=8,'shard_0'=4,'shard_1'=4,'shard_2'=2] {'shard_2'}, dimensions={0} | all-to-all | bytes 8388608 | tf_op jit(solution)/shard_map/all_to_all | solution.py:24
  20.9 5.2 %reduce_sum.30 = bf16[16,64,1024]{2,1,0:T(8,128)(2,1)} reduce(bf16[2,16,64,1024]{3,2,1,0:T(8,128)(2,1)} %all_to_all.25, bf16[]{:T(256)} %constant.4.clone.1), dimensions={0}, to_apply=%region_0.0 | reduce | flops 1048576 | bytes 6291458 | tf_op jit(solution)/shard_map/reduce_sum | solution.py:25
  26.1 0.0 copy-start.1
  26.1 58.0 %all_to_all.26 = bf16[16,64,1024]{2,1,0:T(8,128)(2,1)S(1)} all-to-all(bf16[16,64,1024]{2,1,0:T(8,128)(2,1)} %reduce_sum.30), channel_id=1, replica_groups=mesh['rep'=8,'shard_0'=4,'shard_1'=4,'shard_2'=2] {'shard_0','shard_1'}, dimensions={0} | all-to-all | bytes 4194304 | tf_op jit(solution)/shard_map/all_to_all | solution.py:32
  84.2 0.4 convert_reduce_fusion
  84.6 0.0 copy-done.1
  84.6 0.0 copy-done.2
  84.6 0.0 copy-done.3
  84.6 0.1 fusion.1
  84.8 0.0 copy-start.4
  84.8 0.2 broadcast_in_dim.6
  85.0 31.8 %all_to_all.27 = f32[8,64,1024]{2,1,0:T(8,128)} all-to-all(f32[8,64,1024]{2,1,0:T(8,128)S(1)} %broadcast_in_dim.6), channel_id=1, replica_groups=mesh['rep'=8,'shard_0'=4,'shard_1'=4,'shard_2'=2] {'rep'}, dimensions={0} | all-to-all | bytes 4194304 | tf_op jit(solution)/shard_map/all_to_all | solution.py:38
  116.8 1.7 reduce_sum.32
  118.6 0.0 copy-done.4
  118.6 0.9 fusion.2
  119.4 0.2 broadcast_in_dim.7
  119.7 54.6 %all_to_all.28 = bf16[16,64,1024]{2,1,0:T(8,128)(2,1)S(1)} all-to-all(bf16[16,64,1024]{2,1,0:T(8,128)(2,1)S(1)} %broadcast_in_dim.7), channel_id=1, replica_groups=mesh['rep'=8,'shard_0'=4,'shard_1'=4,'shard_2'=2] {'shard_0','shard_1'}, dimensions={0} | all-to-all | bytes 4194304 | tf_op jit(solution)/shard_map/all_to_all | solution.py:38
  174.3 0.6 broadcast_in_dim.8
  174.9 8.9 %all_to_all.29 = bf16[2,16,64,1024]{3,2,1,0:T(8,128)(2,1)S(1)} all-to-all(bf16[2,16,64,1024]{3,2,1,0:T(8,128)(2,1)S(1)} %broadcast_in_dim.8), channel_id=1, replica_groups=mesh['rep'=8,'shard_0'=4,'shard_1'=4,'shard_2'=2] {'shard_2'}, dimensions={0} | all-to-all | bytes 8388608 | tf_op jit(solution)/shard_map/all_to_all | solution.py:38
  183.8 2.5 %copy.13 = bf16[2,16,64,1024]{3,2,0,1:T(8,128)(2,1)} copy(bf16[2,16,64,1024]{3,2,1,0:T(8,128)(2,1)S(1)} %all_to_all.29) | data formatting | bytes 8388608 | tf_op jit(solution)/shard_map/all_to_all | solution.py:38
  (2 shorter events, 0.0 us)
Async XLA Ops:
  0.6 1.6 copy-start
  26.1 58.5 %copy-start.1 = (f32[64,1024]{1,0:T(8,128)S(1)}, f32[64,1024]{1,0:T(8,128)}, u32[]{:S(2)}) copy-start(f32[64,1024]{1,0:T(8,128)} %param.10) | copy-start | bytes 786436
  26.1 58.5 %copy-start.2 = (f32[1,64,1024]{2,1,0:T(8,128)S(1)}, f32[1,64,1024]{2,1,0:T(8,128)}, u32[]{:S(2)}) copy-start(f32[1,64,1024]{2,1,0:T(8,128)} %param.8) | copy-start | bytes 786436
  26.1 58.5 %copy-start.3 = (f32[1,64,1024]{2,1,0:T(8,128)S(1)}, f32[1,64,1024]{2,1,0:T(8,128)}, u32[]{:S(2)}) copy-start(f32[1,64,1024]{2,1,0:T(8,128)} %param.9) | copy-start | bytes 786436
  84.8 33.8 %copy-start.4 = (f32[64,1024]{1,0:T(8,128)S(1)}, f32[64,1024]{1,0:T(8,128)}, u32[]{:S(2)}) copy-start(f32[64,1024]{1,0:T(8,128)} %param.11) | copy-start | bytes 786436
where the time goes:
time: 187 us; the launch traced here: 186 us
  blocking collectives  164 us (88%)
  other arithmetic  8.35 us (4%)
  matrix products  6.99 us (4%)
  local copies, waits for them, and re-layouts  5.88 us (3%)
    all_to_all x3, blocking collectives, copy_for_each(): lax.all_to_all(jnp.broadcast_to(array[None], (length, *array.shape)), axi...  95.3 us
    all_to_all x1, blocking collectives, summed_rows(): lax.all_to_all(own.astype(jnp.bfloat16), far, 0, 0, tiled=True)  58 us
    all_to_all x1, blocking collectives, sum_at_owner(): lax.all_to_all(cut_along(array, dim, length), axis, 0, 0, tiled=True)  11 us
    dot_general x1, matrix products, per_device(): lax.dot_general(activations, cotangents, (((0,), (0,)), ((), ())), prefer...  6.99 us
    reduce_sum x1, other arithmetic, sum_at_owner(): return jnp.sum(blocks.astype(jnp.float32), axis=0)  5.2 us

commit v1 on v0

v1 whole, which is shorter than its diff:
```python
import functools

import jax
import jax.numpy as jnp
from jax import lax
from jax.experimental import pallas as pl
from jax.experimental.pallas import tpu as pltpu
from jax.sharding import Mesh
from jax.sharding import PartitionSpec as P

MESH = pl.DeviceIdType.MESH
AXES = ("zl", "y", "zh", "x", "c")
SIZE = {"zl": 2, "y": 4, "zh": 4, "x": 4, "c": 2}
REP = ("zl", "y")
SHARD = ("zh", "x", "c")
BF16, F32 = jnp.bfloat16, jnp.float32

outer_rate = 0.7
inertia = 0.9
inner_rate = 0.3
epsilon = 1e-08

NQ = 2
SEMS = 96


def kernel(
    act, cot, inner, moment, outer, mom, new_p, new_m, cc,
    a_buf, b_buf, grad, core_in, two_in, direct_in, fwd_in, weight, y_own, y_in, z_own, z_in,
    base, base_in, base_sum, base_y, nm, load_sem, ss, rs,
):
    zl, y, zh, x, c = (lax.axis_index(a) for a in AXES)
    at = {"zl": zl, "y": y, "zh": zh, "x": x, "c": c}

    def shift(axis, d):
        return {axis: lax.rem(at[axis] + d, SIZE[axis])}

    z = zh * 2 + zl

    def z_shift(d):
        there = lax.rem(z + d, 8)
        return {"zh": there // 2, "zl": lax.rem(there, 2)}

    core = {"c": 1 - c}
    pair = {"zl": 1 - zl}

    loads = [pltpu.make_async_copy(cot, b_buf, load_sem.at[16])]
    steps = (2, 1, 3, 0)
    for j, step in enumerate(steps):
        there = lax.rem(x + step, 4)
        for h in range(4):
            columns = pl.ds(pl.multiple_of(h * 512 + there * 128, 128), 128)
            loads.append(
                pltpu.make_async_copy(
                    act.at[:, columns], a_buf.at[j, :, pl.ds(h * 128, 128)], load_sem.at[j * 4 + h]
                )
            )
    for load in loads:
        load.start()

    barrier = pltpu.get_barrier_semaphore()
    peers = [core] + [shift("x", d) for d in (1, 2, 3)] + [shift("y", d) for d in (1, 2, 3)]
    peers += [z_shift(d) for d in range(1, 8)]
    for peer in peers:
        pl.semaphore_signal(barrier, inc=1, device_id=peer, device_id_type=MESH)

    factor = (inner_rate / (8 * 32768)) / (jnp.sqrt(moment[0]) + epsilon)
    for q in range(NQ):
        weight[q, zh] = factor[q * 32 : q * 32 + 32].astype(BF16)
    for t in range(4):
        for s in range(2):
            cols = slice(t * 256 + s * 128, t * 256 + s * 128 + 128)
            base[s, t] = outer[:, cols] - inner[0, :, cols]

    pl.semaphore_wait(barrier, len(peers))

    count = [0]
    sent = []

    def send(src, dst, peer):
        i = count[0]
        count[0] += 1
        copy = pltpu.make_async_remote_copy(
            src, dst, ss.at[i], rs.at[i], device_id=peer, device_id_type=MESH
        )
        copy.start()
        sent.append(copy)
        return copy

    w_copies = [send(weight.at[:, zh], weight.at[:, zh], shift("zh", d)) for d in (1, 2, 3)]
    base_copy = send(base.at[1 - zl], base_in, pair)

    core_copies = []
    loads[0].wait()

    def product(j):
        for load in loads[1 + 4 * j : 5 + 4 * j]:
            load.wait()
        for n in range(2):
            cols = slice(n * 512, n * 512 + 512)
            value = lax.dot_general(
                a_buf[j], b_buf[:, cols], (((0,), (0,)), ((), ())), preferred_element_type=F32
            ).astype(BF16)
            for h in range(4):
                for k in range(2):
                    for q in range(NQ):
                        row = h * 128 + k * 64 + q * 32
                        grad[j, k, q, h, :, cols] = value[row : row + 32]
        core_copies.append(send(grad.at[j, 1 - c], core_in.at[j], core))

    def chip_sum(j):
        core_copies[j].wait_recv()
        for q in range(NQ):
            for h in range(4):
                grad[j, c, q, h] = grad[j, c, q, h] + core_in[j, q, h]

    lo, hi = pl.ds(0, 2), pl.ds(2, 2)
    right, left = shift("x", 1), shift("x", 3)
    two, direct, fwd = {}, {}, {}

    def send_two(q):
        two[q] = (
            send(grad.at[0, c, q, lo], two_in.at[q, 0], left),
            send(grad.at[0, c, q, hi], two_in.at[q, 1], right),
        )

    def send_right(q):
        direct[q, 0] = send(grad.at[1, c, q, lo], direct_in.at[q, 0], right)

    def send_left(q):
        direct[q, 1] = send(grad.at[2, c, q, hi], direct_in.at[q, 1], left)

    def forward(q):
        two[q][1].wait_recv()
        for h in range(2):
            grad[1, c, q, 2 + h] = grad[1, c, q, 2 + h] + two_in[q, 1, h]
        right_copy = send(grad.at[1, c, q, hi], fwd_in.at[q, 1], right)
        two[q][0].wait_recv()
        for h in range(2):
            grad[2, c, q, h] = grad[2, c, q, h] + two_in[q, 0, h]
        fwd[q] = (send(grad.at[2, c, q, lo], fwd_in.at[q, 0], left), right_copy)

    y_copies = {}

    def finish_x(q):
        for copy in (direct[q, 0], direct[q, 1], *fwd[q]):
            copy.wait_recv()
        for h in range(4):
            half, place = h // 2, h % 2
            total = grad[3, c, q, h].astype(F32) + direct_in[q, half, place].astype(F32)
            total = total + fwd_in[q, half, place].astype(F32)
            total = (total * weight[q, h].astype(F32)).astype(BF16)
            for t in range(4):
                y_own[q, t, h] = total[:, t * 256 : t * 256 + 256]
        y_copies[q] = [
            send(y_own.at[q, lax.rem(y + d, 4)], y_in.at[q, d - 1], shift("y", d)) for d in (1, 3, 2)
        ]

    z_copies = {}

    def finish_y(q):
        for copy in y_copies[q]:
            copy.wait_recv()
        for h in range(4):
            total = y_own[q, y, h].astype(F32) + y_in[q, 0, h].astype(F32)
            total = total + y_in[q, 1, h].astype(F32) + y_in[q, 2, h].astype(F32)
            for s in range(2):
                z_own[q, h * 2 + s] = total[:, s * 128 : s * 128 + 128].astype(BF16)
        z_copies[q] = [
            send(z_own.at[q, lax.rem(z + d, 8)], z_in.at[q, d - 1], z_shift(d))
            for d in (4, 3, 5, 2, 6, 1, 7)
        ]

    product(0)
    product(1)
    chip_sum(0)
    two_sent = send_two(0)
    product(2)
    chip_sum(1)
    send_right(0)
    product(3)
    chip_sum(2)
    send_left(0)
    base_copy.wait_recv()
    for t in range(4):
        base_sum[t] = base[zl, t] + base_in[t]
    base_copies = [
        send(base_sum.at[lax.rem(y + d, 4)], base_y.at[d - 1], shift("y", d)) for d in (1, 2, 3)
    ]
    chip_sum(3)
    forward(0)
    send_two(1)
    send_right(1)
    send_left(1)
    for copy in w_copies:
        copy.wait_recv()
    finish_x(0)
    for copy in base_copies:
        copy.wait_recv()
    pseudo_base = base_sum[y] + base_y[0] + base_y[1] + base_y[2]
    forward(1)
    finish_y(0)
    finish_x(1)
    finish_y(1)

    cut = pl.ds(pl.multiple_of(y * 256 + zl * 128, 128), 128)
    y_cut = pl.ds(pl.multiple_of(y * 256, 128), 256)
    for q in range(NQ):
        for copy in z_copies[q]:
            copy.wait_recv()
        rows = pl.ds(q * 32, 32)
        total = z_own[q, z].astype(F32)
        for d in range(7):
            total = total + z_in[q, d].astype(F32)
        pseudo = pseudo_base[q * 32 : q * 32 + 32] / 8 + total
        fresh_m = inertia * mom[rows, cut] + pseudo
        fresh_p = outer[rows, cut] - outer_rate * (pseudo + inertia * fresh_m)
        cc[zh, x, c, rows, cut] = fresh_p.astype(BF16)
        nm[rows, cut] = fresh_m.astype(BF16)

    own = cc.at[zh, x, c, :, cut]
    far = [send(own, own, z_shift(d)) for d in (4, 3, 5, 2, 6, 1, 7)]
    nm_pair = send(nm.at[:, cut], nm.at[:, cut], pair)
    for copy in far:
        copy.wait_recv()
    rows0, rows1 = pl.ds(0, 32), pl.ds(32, 32)
    part0 = cc.at[:, x, c, rows0, y_cut]
    part1 = cc.at[:, x, c, rows1, y_cut]
    mid0 = [send(part0, part0, shift("y", d)) for d in (1, 3, 2)]
    mid1 = [send(part1, part1, shift("x", d)) for d in (1, 3, 2)]
    nm_pair.wait_recv()
    nm_y = [send(nm.at[:, y_cut], nm.at[:, y_cut], shift("y", d)) for d in (1, 3, 2)]

    up, down = shift("y", 1), shift("y", 3)
    last = []

    def core_send(part):
        last.append(send(part, part, core))

    def x_part(place, rows):
        return cc.at[:, place, c, rows]

    def y_part(place, rows):
        return cc.at[:, :, c, rows, pl.ds(pl.multiple_of(place * 256, 128), 256)]

    for copy in mid0:
        copy.wait_recv()
    mine0 = x_part(x, rows0)
    ring0 = [send(mine0, mine0, right), send(mine0, mine0, left)]
    for copy in mid1:
        copy.wait_recv()
    mine1 = y_part(y, rows1)
    ring1 = [send(mine1, mine1, up), send(mine1, mine1, down)]
    core_send(mine0)
    core_send(mine1)
    x_left, x_right = lax.rem(x + 3, 4), lax.rem(x + 1, 4)
    y_down, y_up = lax.rem(y + 3, 4), lax.rem(y + 1, 4)
    ring0[0].wait_recv()
    piece = x_part(x_left, pl.ds(0, 16))
    tail = [send(piece, piece, right)]
    ring0[1].wait_recv()
    piece = x_part(x_right, pl.ds(16, 16))
    tail.append(send(piece, piece, left))
    ring1[0].wait_recv()
    piece = y_part(y_down, pl.ds(32, 16))
    tail.append(send(piece, piece, up))
    ring1[1].wait_recv()
    piece = y_part(y_up, pl.ds(48, 16))
    tail.append(send(piece, piece, down))
    core_send(x_part(x_left, rows0))
    core_send(x_part(x_right, rows0))
    core_send(y_part(y_down, rows1))
    core_send(y_part(y_up, rows1))
    for copy in nm_y:
        copy.wait_recv()
    new_m[...] = nm[...].astype(F32)
    x_far, y_far = lax.rem(x + 2, 4), lax.rem(y + 2, 4)
    tail[0].wait_recv()
    core_send(x_part(x_far, pl.ds(0, 16)))
    tail[1].wait_recv()
    core_send(x_part(x_far, pl.ds(16, 16)))
    tail[2].wait_recv()
    core_send(y_part(y_far, pl.ds(32, 16)))
    tail[3].wait_recv()
    core_send(y_part(y_far, pl.ds(48, 16)))
    new_p[...] = cc[zh, x, c].astype(F32)
    for copy in last:
        copy.wait_recv()
    for copy in sent:
        copy.wait_send()


def per_device(activations, cotangents, inner_params, inner_moment, outer_params, momentum):
    vmem = pl.BlockSpec(memory_space=pltpu.VMEM)
    hbm = pl.BlockSpec(memory_space=pl.ANY)
    new_p, new_m, cc = pl.pallas_call(
        kernel,
        out_shape=(
            jax.ShapeDtypeStruct((64, 1024), F32),
            jax.ShapeDtypeStruct((64, 1024), F32),
            jax.ShapeDtypeStruct((4, 4, 2, 64, 1024), BF16),
        ),
        in_specs=[hbm, hbm, vmem, vmem, vmem, vmem],
        out_specs=(vmem, vmem, vmem),
        scratch_shapes=[
            pltpu.VMEM((4, 1024, 512), BF16),
            pltpu.VMEM((1024, 1024), BF16),
            pltpu.VMEM((4, 2, NQ, 4, 32, 1024), BF16),
            pltpu.VMEM((4, NQ, 4, 32, 1024), BF16),
            pltpu.VMEM((NQ, 2, 2, 32, 1024), BF16),
            pltpu.VMEM((NQ, 2, 2, 32, 1024), BF16),
            pltpu.VMEM((NQ, 2, 2, 32, 1024), BF16),
            pltpu.VMEM((NQ, 4, 32, 1024), BF16),
            pltpu.VMEM((NQ, 4, 4, 32, 256), BF16),
            pltpu.VMEM((NQ, 3, 4, 32, 256), BF16),
            pltpu.VMEM((NQ, 8, 32, 128), BF16),
            pltpu.VMEM((NQ, 7, 32, 128), BF16),
            pltpu.VMEM((2, 4, 64, 128), F32),
            pltpu.VMEM((4, 64, 128), F32),
            pltpu.VMEM((4, 64, 128), F32),
            pltpu.VMEM((3, 64, 128), F32),
            pltpu.VMEM((64, 1024), BF16),
            pltpu.SemaphoreType.DMA((17,)),
            pltpu.SemaphoreType.DMA((SEMS,)),
            pltpu.SemaphoreType.DMA((SEMS,)),
        ],
        compiler_params=pltpu.CompilerParams(
            collective_id=0, has_side_effects=True, vmem_limit_bytes=56 * 2**20
        ),
    )(activations, cotangents, inner_params, inner_moment, outer_params, momentum)
    return new_p, new_m, cc.reshape(2048, 1024)


def solution(mesh):
    split = Mesh(mesh.devices.reshape(*(SIZE[a] for a in AXES)), AXES)
    return jax.shard_map(
        per_device,
        mesh=split,
        in_specs=(
            P(AXES, None),
            P(AXES, None),
            P(REP, SHARD, None),
            P(REP, SHARD, None),
            P(SHARD, None),
            P(SHARD, None),
        ),
        out_specs=(P(SHARD, None), P(SHARD, None), P()),
        check_vma=False,
    )
```

time: 187 us -> 87.5 us (0.47)
  blocking collectives: 164 us -> 0 us
  Pallas kernels: 0 us -> 78.7 us
  other arithmetic: 8.35 us -> 0 us
  matrix products: 6.99 us -> 0 us
  local copies, waits for them, and re-layouts: 5.88 us -> 7.98 us
    all_to_all x5 -> x0, blocking collectives: 164 us -> none  [the longest x3 95.3 us: copy_for_each(): lax.all_to_all(jnp.broadcast_to(array[None], (length, *array.shape)), axi...]
    pallas_call x0 -> x1, Pallas kernels: none -> 78.7 us  [per_device(): pl.pallas_call(kernel, out_shape=(jax.ShapeDtypeStruct((64, 1024), F32),...]
    reduce_sum x3 -> x0, other arithmetic: 7.34 us -> none  [the longest x1 5.2 us: sum_at_owner(): return jnp.sum(blocks.astype(jnp.float32), axis=0)]
    dot_general x1 -> x0, matrix products: 6.99 us -> none  [per_device(): lax.dot_general(activations, cotangents, (((0,), (0,)), ((), ())), prefer...]
    unnamed x10 -> x3, local copies, waits for them, and re-layouts: 1.61 us -> 7.98 us
    all_to_all x1 -> x0, local copies, waits for them, and re-layouts: 2.45 us -> none  [copy_for_each(): lax.all_to_all(jnp.broadcast_to(array[None], (length, *array.shape)), axi...]
where the time goes in v1:
time: 87.5 us; the launch traced here: 87.3 us
  Pallas kernels  78.7 us (90%)
  local copies, waits for them, and re-layouts  7.98 us (9%)
    pallas_call x1, Pallas kernels, per_device(): pl.pallas_call(kernel, out_shape=(jax.ShapeDtypeStruct((64, 1024), F32),...  78.7 us
    unnamed x3, local copies, waits for them, and re-layouts  7.98 us

profile of v1, /device:TPU:1, one launch (start us, length us, event | category | flops | bytes accessed | tf_op | source)
XLA Modules:
  0.0 87.3 jit_solution(6691499084243332047)
XLA Ops:
  0.6 78.7 %shard_map.85 = (f32[64,1024]{1,0:T(8,128)}, f32[64,1024]{1,0:T(8,128)}, bf16[4,4,2,64,1024]{4,3,2,1,0:T(8,128)(2,1)}) custom-call(bf16[1024,2048]{1,0:T(8,128)(2,1)} %act.1, bf16[1024,1024]{1,0:T(8,128)(2,1)} %cot.1, f32[1,64,1024]{2,1,0:T(8,128)} %inner.1, f32[1,64,1024]{2,1,0:T(8,128)} %moment.1, f32[64,1024]{1,0:T(8,128)} %outer.1, f32[64,1024]{1,0:T(8,128)} %mom.1), custom_call_target="tpu_custom_call" | custom-call | tf_op jit(solution)/shard_map/pallas_call | solution.py:296
  79.3 1.7 %copy.12 = f32[64,1024]{1,0:T(8,128)} copy(f32[64,1024]{1,0:T(8,128)} %get-tuple-element.12) | data formatting | bytes 524288
  81.0 1.7 %copy.13 = f32[64,1024]{1,0:T(8,128)} copy(f32[64,1024]{1,0:T(8,128)} %get-tuple-element.13) | data formatting | bytes 524288
  82.6 4.6 %copy.14 = bf16[2048,1024]{1,0:T(8,128)(2,1)} copy(bf16[2048,1024]{1,0:T(8,128)(2,1)} %bitcast.1) | data formatting | bytes 8388608

commit v2 on v0

v2 whole, which is shorter than its diff:
```python
import functools

import jax
import jax.numpy as jnp
from jax import lax
from jax.experimental import pallas as pl
from jax.experimental.pallas import tpu as pltpu
from jax.sharding import Mesh
from jax.sharding import PartitionSpec as P

MESH = pl.DeviceIdType.MESH
AXES = ("zl", "y", "zh", "x", "c")
SIZE = {"zl": 2, "y": 4, "zh": 4, "x": 4, "c": 2}
REP = ("zl", "y")
SHARD = ("zh", "x", "c")
BF16, F32 = jnp.bfloat16, jnp.float32

outer_rate = 0.7
inertia = 0.9
inner_rate = 0.3
epsilon = 1e-08

NQ = 4
COLS = 1024 // NQ
SEMS = 200
STEPS = (2, 1, 3, 0)
FAR = (4, 3, 5, 2, 6, 1, 7)


def kernel(
    act, cot, inner_h, moment_h, outer_h, mom_h, nm, cc,
    a_buf, b_buf, grad, core_in, two_in, direct_in, fwd_in, weight, y_own, y_in, z_own, z_in,
    inner, moment, outer, mom, base, base_in, base_sum, base_y, load_sem, ss, rs,
):
    zl, y, zh, x, c = (lax.axis_index(a) for a in AXES)
    at = {"zl": zl, "y": y, "zh": zh, "x": x, "c": c}

    def shift(axis, d):
        return {axis: lax.rem(at[axis] + d, SIZE[axis])}

    z = zh * 2 + zl

    def z_shift(d):
        there = lax.rem(z + d, 8)
        return {"zh": there // 2, "zl": lax.rem(there, 2)}

    core = {"c": 1 - c}
    pair = {"zl": 1 - zl}
    right, left = shift("x", 1), shift("x", 3)

    barrier = pltpu.get_barrier_semaphore()
    peers = [core] + [shift("x", d) for d in (1, 2, 3)] + [shift("y", d) for d in (1, 2, 3)]
    peers += [z_shift(d) for d in range(1, 8)]
    for peer in peers:
        pl.semaphore_signal(barrier, inc=1, device_id=peer, device_id_type=MESH)

    loads = []

    def load(src, dst):
        copy = pltpu.make_async_copy(src, dst, load_sem.at[len(loads)])
        copy.start()
        loads.append(copy)

    a_loads, b_loads = {}, {}

    def load_a(j):
        there = lax.rem(x + STEPS[j], 4)
        for h in range(4):
            columns = pl.ds(pl.multiple_of(h * 512 + there * 128, 128), 128)
            load(act.at[:, columns], a_buf.at[j, :, pl.ds(h * 128, 128)])
        a_loads[j] = loads[-4:]

    def load_b(p):
        load(cot.at[:, pl.ds(p * 512, 512)], b_buf.at[p])
        b_loads[p] = loads[-1:]

    load_a(0)
    load_b(0)
    load_a(1)
    load_a(2)
    load(moment_h, moment)
    moment_load = loads[-1]
    load(inner_h, inner)
    load(outer_h, outer)
    base_loads = loads[-2:]
    load_a(3)
    load_b(1)
    load(mom_h, mom)
    mom_load = loads[-1]

    count = [0]
    sent = []

    def send(src, dst, peer):
        i = count[0]
        count[0] += 1
        copy = pltpu.make_async_remote_copy(
            src, dst, ss.at[i], rs.at[i], device_id=peer, device_id_type=MESH
        )
        copy.start()
        sent.append(copy)
        return copy

    def arrive(copies):
        for copy in copies:
            copy.wait_recv()

    core_copies = {}

    def product(j, p):
        for copy in a_loads.pop(j, []) + b_loads.pop(p, []):
            copy.wait()
        value = lax.dot_general(
            a_buf[j], b_buf[p], (((0,), (0,)), ((), ())), preferred_element_type=F32
        ).astype(BF16)
        for q in range(2):
            for h in range(4):
                for k in range(2):
                    row = h * 128 + k * 64
                    part = value[row : row + 64, q * COLS : q * COLS + COLS]
                    grad[j, k, 2 * p + q, h] = part

    def core_share(j, p):
        for q in (2 * p, 2 * p + 1):
            core_copies[j, q] = send(grad.at[j, 1 - c, q], core_in.at[j, q], core)

    def chip_sum(j, q):
        core_copies[j, q].wait_recv()
        for h in range(4):
            grad[j, c, q, h] = grad[j, c, q, h] + core_in[j, q, h]

    lo, hi = pl.ds(0, 2), pl.ds(2, 2)
    two, direct, fwd, y_copies, z_copies = {}, {}, {}, {}, {}
    far, mid0, mid1, last0, last1 = {}, {}, {}, {}, {}

    def send_two(q):
        two[q] = (
            send(grad.at[0, c, q, lo], two_in.at[q, 0], left),
            send(grad.at[0, c, q, hi], two_in.at[q, 1], right),
        )

    def send_right(q):
        direct[q, 0] = send(grad.at[1, c, q, lo], direct_in.at[q, 0], right)

    def send_left(q):
        direct[q, 1] = send(grad.at[2, c, q, hi], direct_in.at[q, 1], left)

    def forward(q):
        two[q][1].wait_recv()
        for h in range(2):
            grad[1, c, q, 2 + h] = grad[1, c, q, 2 + h] + two_in[q, 1, h]
        right_copy = send(grad.at[1, c, q, hi], fwd_in.at[q, 1], right)
        two[q][0].wait_recv()
        for h in range(2):
            grad[2, c, q, h] = grad[2, c, q, h] + two_in[q, 0, h]
        fwd[q] = (send(grad.at[2, c, q, lo], fwd_in.at[q, 0], left), right_copy)

    def finish_x(q):
        arrive(w_copies[q])
        arrive((direct[q, 0], direct[q, 1], *fwd[q]))
        for h in range(4):
            half, place = h // 2, h % 2
            total = grad[3, c, q, h].astype(F32) + direct_in[q, half, place].astype(F32)
            total = total + fwd_in[q, half, place].astype(F32)
            total = (total * weight[q, h].astype(F32)).astype(BF16)
            for t in range(4):
                y_own[q, t, h] = total[t * 16 : t * 16 + 16]
        y_copies[q] = [
            send(y_own.at[q, lax.rem(y + d, 4)], y_in.at[q, d - 1], shift("y", d)) for d in (2, 1, 3)
        ]

    def finish_y(q):
        arrive(y_copies[q])
        for h in range(4):
            total = y_own[q, y, h].astype(F32) + y_in[q, 0, h].astype(F32)
            total = total + y_in[q, 1, h].astype(F32) + y_in[q, 2, h].astype(F32)
            for s in range(2):
                z_own[q, h * 2 + s] = total[:, s * 128 : s * 128 + 128].astype(BF16)
        z_copies[q] = [
            send(z_own.at[q, lax.rem(z + d, 8)], z_in.at[q, d - 1], z_shift(d)) for d in FAR
        ]

    rows = pl.ds(pl.multiple_of(y * 16, 16), 16)

    def finish_z(q):
        arrive(z_copies[q])
        cut = pl.ds(pl.multiple_of(q * COLS + zl * 128, 128), 128)
        total = z_own[q, z].astype(F32)
        for d in range(7):
            total = total + z_in[q, d].astype(F32)
        pseudo = base_y[3, :, q * 128 : q * 128 + 128] / 8 + total
        fresh_m = inertia * mom[rows, cut] + pseudo
        fresh_p = outer[rows, cut] - outer_rate * (pseudo + inertia * fresh_m)
        cc[zh, x, c, rows, cut] = fresh_p.astype(BF16)
        nm[y, zl, :, q * 128 : q * 128 + 128] = fresh_m.astype(BF16)
        own = cc.at[zh, x, c, rows, cut]
        far[q] = [send(own, own, z_shift(d)) for d in FAR]

    def columns_of(q):
        return pl.ds(q * COLS, COLS)

    def gather_mid(q):
        arrive(far[q])
        part0 = cc.at[lo, x, c, rows, columns_of(q)]
        part1 = cc.at[hi, x, c, rows, columns_of(q)]
        mid0[q] = [send(part0, part0, shift("y", d)) for d in (2, 1, 3)]
        mid1[q] = [send(part1, part1, shift("x", d)) for d in (2, 1, 3)]

    def x_part(q, d):
        return cc.at[lo, lax.rem(x + d, 4), c, :, columns_of(q)]

    def y_part(q, d):
        place = pl.ds(pl.multiple_of(lax.rem(y + d, 4) * 16, 16), 16)
        return cc.at[hi, :, c, place, columns_of(q)]

    shared = []

    def core_send(part):
        shared.append(send(part, part, core))

    def gather_last(q):
        arrive(mid0[q])
        part0 = x_part(q, 0)
        last0[q] = [(d, send(part0, part0, shift("x", d))) for d in (2, 1, 3)]
        arrive(mid1[q])
        part1 = y_part(q, 0)
        last1[q] = [(d, send(part1, part1, shift("y", d))) for d in (2, 1, 3)]
        if q == NQ - 1:
            core_send(part0)
            core_send(part1)

    def gather_core(q):
        if q < NQ - 1:
            arrive([copy for _, copy in last0[q] + last1[q]])
            core_send(cc.at[:, :, c, :, columns_of(q)])
            return
        for i in (1, 2, 0):
            d, copy = last0[q][i]
            copy.wait_recv()
            core_send(x_part(q, 4 - d))
            d, copy = last1[q][i]
            copy.wait_recv()
            core_send(y_part(q, 4 - d))

    def make(*pairs):
        for j, p in pairs:
            product(j, p)
            core_share(j, p)

    product(0, 0)
    pl.semaphore_wait(barrier, len(peers))
    core_share(0, 0)
    make((1, 0))
    chip_sum(0, 0)
    send_two(0)
    chip_sum(0, 1)
    send_two(1)
    make((2, 0))
    chip_sum(1, 0)
    send_right(0)
    moment_load.wait()
    factor = (inner_rate / (8 * 32768)) / (jnp.sqrt(moment[0]) + epsilon)
    w_copies = {}

    def share_weight(q):
        part = weight.at[q, zh]
        w_copies[q] = [send(part, part, shift("zh", d)) for d in (2, 1, 3)]

    for q in range(NQ):
        weight[q, zh] = factor[:, q * COLS : q * COLS + COLS].astype(BF16)
    share_weight(0)
    for copy in base_loads:
        copy.wait()
    for t in range(4):
        for s in range(2):
            for q in range(NQ):
                cols = slice(q * COLS + s * 128, q * COLS + s * 128 + 128)
                part = slice(t * 16, t * 16 + 16)
                base[s, t, :, q * 128 : q * 128 + 128] = outer[part, cols] - inner[0, part, cols]
    base_copy = send(base.at[1 - zl], base_in, pair)
    for q in range(1, NQ):
        share_weight(q)
    chip_sum(2, 0)
    send_left(0)
    make((3, 0), (0, 1))
    for j in (1, 2, 3):
        chip_sum(j, 1)
    chip_sum(3, 0)
    forward(0)
    chip_sum(0, 2)
    send_two(2)
    send_right(1)
    send_left(1)
    make((1, 1))
    forward(1)
    chip_sum(0, 3)
    send_two(3)
    make((2, 1))
    chip_sum(1, 2)
    send_right(2)
    make((3, 1))
    chip_sum(2, 2)
    send_left(2)
    for j, q in ((3, 2), (1, 3), (2, 3), (3, 3)):
        chip_sum(j, q)
    mom_load.wait()

    held = {}

    def base_pair():
        base_copy.wait_recv()
        for t in range(4):
            base_sum[t] = base[zl, t] + base_in[t]
        held["base"] = [
            send(base_sum.at[lax.rem(y + d, 4)], base_y.at[d - 1], shift("y", d)) for d in (2, 1, 3)
        ]

    def base_total():
        arrive(held["base"])
        base_y[3] = base_sum[y] + base_y[0] + base_y[1] + base_y[2]

    def fwd_and_next(q):
        forward(q)
        if q == 2:
            send_right(3)
            send_left(3)

    def nm_pair():
        part = nm.at[y, zl]
        held["nm"] = send(part, part, pair)

    def nm_y():
        held["nm"].wait_recv()
        part = nm.at[y]
        held["nm_y"] = [send(part, part, shift("y", d)) for d in (2, 1, 3)]

    done = (7.6, 11.8, 16.0, 19.0)
    events = [(9.0, fwd_and_next, (2,)), (13.2, fwd_and_next, (3,))]
    events += [(11.3, base_pair, ()), (15.5, base_total, ())]
    stages = (finish_x, finish_y, finish_z, gather_mid, gather_last, gather_core)
    for q in range(NQ):
        waits = (0, 3.5, 8, 12.5, 16, 22) if q < NQ - 1 else (0, 3, 6.8, 10.5, 13.5, 18.5)
        events += [(done[q] + wait, stage, (q,)) for wait, stage in zip(waits, stages)]
    events += [(done[-1] + 7.1, nm_pair, ()), (done[-1] + 11.1, nm_y, ())]
    for _, stage, operands in sorted(events, key=lambda event: event[0]):
        stage(*operands)
    arrive(held["nm_y"])
    arrive(shared)
    for copy in sent:
        copy.wait_send()


def write(nm, cc, new_p, new_m, out, buf_p, buf_m, sem):
    zh, x, c = (lax.axis_index(a) for a in SHARD)
    copies = [pltpu.make_async_copy(cc, out, sem.at[0])]
    copies[0].start()
    buf_p[...] = cc[zh, x, c].astype(F32)
    copies.append(pltpu.make_async_copy(buf_p, new_p, sem.at[1]))
    copies[1].start()
    for t in range(4):
        for s in range(2):
            for q in range(NQ):
                cols = slice(q * COLS + s * 128, q * COLS + s * 128 + 128)
                value = nm[t, s, :, q * 128 : q * 128 + 128].astype(F32)
                buf_m[t * 16 : t * 16 + 16, cols] = value
    copies.append(pltpu.make_async_copy(buf_m, new_m, sem.at[2]))
    copies[2].start()
    for copy in copies:
        copy.wait()


def per_device(activations, cotangents, inner_params, inner_moment, outer_params, momentum):
    vmem = pl.BlockSpec(memory_space=pltpu.VMEM)
    hbm = pl.BlockSpec(memory_space=pltpu.HBM)
    whole = (4, 4, 2, 64, 1024)
    nm, cc = pl.pallas_call(
        kernel,
        out_shape=(pltpu.VMEM((4, 2, 16, NQ * 128), BF16), pltpu.VMEM(whole, BF16)),
        in_specs=[hbm] * 6,
        out_specs=(vmem, vmem),
        scratch_shapes=[
            pltpu.VMEM((4, 1024, 512), BF16),
            pltpu.VMEM((2, 1024, 512), BF16),
            pltpu.VMEM((4, 2, NQ, 4, 64, COLS), BF16),
            pltpu.VMEM((4, NQ, 4, 64, COLS), BF16),
            pltpu.VMEM((NQ, 2, 2, 64, COLS), BF16),
            pltpu.VMEM((NQ, 2, 2, 64, COLS), BF16),
            pltpu.VMEM((NQ, 2, 2, 64, COLS), BF16),
            pltpu.VMEM((NQ, 4, 64, COLS), BF16),
            pltpu.VMEM((NQ, 4, 4, 16, COLS), BF16),
            pltpu.VMEM((NQ, 3, 4, 16, COLS), BF16),
            pltpu.VMEM((NQ, 8, 16, 128), BF16),
            pltpu.VMEM((NQ, 7, 16, 128), BF16),
            pltpu.VMEM((1, 64, 1024), F32),
            pltpu.VMEM((1, 64, 1024), F32),
            pltpu.VMEM((64, 1024), F32),
            pltpu.VMEM((64, 1024), F32),
            pltpu.VMEM((2, 4, 16, NQ * 128), F32),
            pltpu.VMEM((4, 16, NQ * 128), F32),
            pltpu.VMEM((4, 16, NQ * 128), F32),
            pltpu.VMEM((4, 16, NQ * 128), F32),
            pltpu.SemaphoreType.DMA((32,)),
            pltpu.SemaphoreType.DMA((SEMS,)),
            pltpu.SemaphoreType.DMA((SEMS,)),
        ],
        compiler_params=pltpu.CompilerParams(
            collective_id=0, has_side_effects=True, vmem_limit_bytes=61100 * 1024
        ),
    )(activations, cotangents, inner_params, inner_moment, outer_params, momentum)
    new_p, new_m, out = pl.pallas_call(
        write,
        out_shape=(
            jax.ShapeDtypeStruct((64, 1024), F32),
            jax.ShapeDtypeStruct((64, 1024), F32),
            jax.ShapeDtypeStruct(whole, BF16),
        ),
        in_specs=[vmem, vmem],
        out_specs=(hbm, hbm, hbm),
        scratch_shapes=[
            pltpu.VMEM((64, 1024), F32),
            pltpu.VMEM((64, 1024), F32),
            pltpu.SemaphoreType.DMA((3,)),
        ],
        compiler_params=pltpu.CompilerParams(vmem_limit_bytes=8 * 2**20),
    )(nm, cc)
    return new_p, new_m, out.reshape(2048, 1024)


def solution(mesh):
    split = Mesh(mesh.devices.reshape(*(SIZE[a] for a in AXES)), AXES)
    return jax.shard_map(
        per_device,
        mesh=split,
        in_specs=(
            P(AXES, None),
            P(AXES, None),
            P(REP, SHARD, None),
            P(REP, SHARD, None),
            P(SHARD, None),
            P(SHARD, None),
        ),
        out_specs=(P(SHARD, None), P(SHARD, None), P()),
        check_vma=False,
    )
```

time: 187 us -> 68.8 us (0.37)
  blocking collectives: 164 us -> 0 us
  Pallas kernels: 0 us -> 68.1 us
  other arithmetic: 8.35 us -> 0 us
  matrix products: 6.99 us -> 0 us
  local copies, waits for them, and re-layouts: 5.88 us -> 0 us
    all_to_all x5 -> x0, blocking collectives: 164 us -> none  [the longest x3 95.3 us: copy_for_each(): lax.all_to_all(jnp.broadcast_to(array[None], (length, *array.shape)), axi...]
    pallas_call x0 -> x2, Pallas kernels: none -> 68.1 us  [the longest x1 65.9 us: per_device(): pl.pallas_call(kernel, out_shape=(pltpu.VMEM((4, 2, 16, NQ * 128), BF16),...]
    reduce_sum x3 -> x0, other arithmetic: 7.34 us -> none  [the longest x1 5.2 us: sum_at_owner(): return jnp.sum(blocks.astype(jnp.float32), axis=0)]
    dot_general x1 -> x0, matrix products: 6.99 us -> none  [per_device(): lax.dot_general(activations, cotangents, (((0,), (0,)), ((), ())), prefer...]
    all_to_all x1 -> x0, local copies, waits for them, and re-layouts: 2.45 us -> none  [copy_for_each(): lax.all_to_all(jnp.broadcast_to(array[None], (length, *array.shape)), axi...]
where the time goes in v2:
time: 68.8 us; the launch traced here: 68.7 us
  Pallas kernels  68.1 us (99%)
    pallas_call x1, Pallas kernels, per_device(): pl.pallas_call(kernel, out_shape=(pltpu.VMEM((4, 2, 16, NQ * 128), BF16),...  65.9 us
    pallas_call x1, Pallas kernels, per_device(): pl.pallas_call(write, out_shape=(jax.ShapeDtypeStruct((64, 1024), F32), j...  2.19 us

profile of v2, /device:TPU:1, one launch (start us, length us, event | category | flops | bytes accessed | tf_op | source)
XLA Modules:
  0.0 68.7 jit_solution(7327875352449012308)
XLA Ops:
  0.6 65.9 %shard_map.85 = (bf16[4,2,16,512]{3,2,1,0:T(8,128)(2,1)S(1)}, bf16[4,4,2,64,1024]{4,3,2,1,0:T(8,128)(2,1)S(1)}) custom-call(bf16[1024,2048]{1,0:T(8,128)(2,1)} %act.1, bf16[1024,1024]{1,0:T(8,128)(2,1)} %cot.1, f32[1,64,1024]{2,1,0:T(8,128)} %inner_h.1, f32[1,64,1024]{2,1,0:T(8,128)} %moment_h.1, f32[64,1024]{1,0:T(8,128)} %outer_h.1, f32[64,1024]{1,0:T(8,128)} %mom_h.1), custom_call_target="tpu_custom_call" | custom-call | tf_op jit(solution)/shard_map/pallas_call | solution.py:376
  66.5 2.2 %shard_map.86 = (f32[64,1024]{1,0:T(8,128)}, f32[64,1024]{1,0:T(8,128)}, bf16[4,4,2,64,1024]{4,3,2,1,0:T(8,128)(2,1)}) custom-call(bf16[4,2,16,512]{3,2,1,0:T(8,128)(2,1)S(1)} %get-tuple-element.8.nm, bf16[4,4,2,64,1024]{4,3,2,1,0:T(8,128)(2,1)S(1)} %get-tuple-element.9.cc), custom_call_target="tpu_custom_call" | custom-call | tf_op jit(solution)/shard_map/pallas_call | solution.py:410

commit v3 on v2

--- a/solution.py
+++ b/solution.py
@@ -22,6 +22,10 @@
 
 NQ = 4
 COLS = 1024 // NQ
+RING = (0, 2, 3)
+FIRST_Z = 1
+ORDER = ("X0", "F3", "Y0", "cs", "zf", "X2", "X3", "Y2", "bt", "Z0", "Y3", "zs", "Z2", "M0", "zx", "Z3", "M2", "L0", "Z1", "np", "M3", "L2", "G0", "M1", "ny", "L3", "G2", "L1", "C0", "C2", "C3", "C1")
+DIRECT = (1, 3)
 SEMS = 200
 STEPS = (2, 1, 3, 0)
 FAR = (4, 3, 5, 2, 6, 1, 7)
@@ -30,7 +34,7 @@
 def kernel(
     act, cot, inner_h, moment_h, outer_h, mom_h, nm, cc,
     a_buf, b_buf, grad, core_in, two_in, direct_in, fwd_in, weight, y_own, y_in, z_own, z_in,
-    inner, moment, outer, mom, base, base_in, base_sum, base_y, load_sem, ss, rs,
+    inner, moment, outer, mom, base, base_in, base_sum, base_far, own_factor, zh_two_in, zh_direct_in, zh_fwd_in, zh_sum, zx_in, rep_own, load_sem, ss, rs,
 ):
     zl, y, zh, x, c = (lax.axis_index(a) for a in AXES)
     at = {"zl": zl, "y": y, "zh": zh, "x": x, "c": c}
@@ -49,8 +53,8 @@
     right, left = shift("x", 1), shift("x", 3)
 
     barrier = pltpu.get_barrier_semaphore()
-    peers = [core] + [shift("x", d) for d in (1, 2, 3)] + [shift("y", d) for d in (1, 2, 3)]
-    peers += [z_shift(d) for d in range(1, 8)]
+    peers = [core, right, left] + [shift("y", d) for d in (1, 2, 3)]
+    peers += [z_shift(d) for d in (1, 2, 6, 7)]
     for peer in peers:
         pl.semaphore_signal(barrier, inc=1, device_id=peer, device_id_type=MESH)
 
@@ -76,10 +80,10 @@
 
     load_a(0)
     load_b(0)
+    load(moment_h, moment)
+    moment_load = loads[-1]
     load_a(1)
     load_a(2)
-    load(moment_h, moment)
-    moment_load = loads[-1]
     load(inner_h, inner)
     load(outer_h, outer)
     base_loads = loads[-2:]
@@ -188,7 +192,7 @@
         total = z_own[q, z].astype(F32)
         for d in range(7):
             total = total + z_in[q, d].astype(F32)
-        pseudo = base_y[3, :, q * 128 : q * 128 + 128] / 8 + total
+        pseudo = base_sum[zl, :, q * 128 : q * 128 + 128] / 8 + total
         fresh_m = inertia * mom[rows, cut] + pseudo
         fresh_p = outer[rows, cut] - outer_rate * (pseudo + inertia * fresh_m)
         cc[zh, x, c, rows, cut] = fresh_p.astype(BF16)
@@ -206,32 +210,52 @@
         mid0[q] = [send(part0, part0, shift("y", d)) for d in (2, 1, 3)]
         mid1[q] = [send(part1, part1, shift("x", d)) for d in (2, 1, 3)]
 
-    def x_part(q, d):
-        return cc.at[lo, lax.rem(x + d, 4), c, :, columns_of(q)]
-
-    def y_part(q, d):
+    def x_part(q, d, blocks=lo):
+        return cc.at[blocks, lax.rem(x + d, 4), c, :, columns_of(q)]
+
+    def y_part(q, d, blocks=hi):
         place = pl.ds(pl.multiple_of(lax.rem(y + d, 4) * 16, 16), 16)
-        return cc.at[hi, :, c, place, columns_of(q)]
+        return cc.at[blocks, :, c, place, columns_of(q)]
 
     shared = []
 
     def core_send(part):
         shared.append(send(part, part, core))
+
+    up, down = shift("y", 1), shift("y", 3)
+    ring0, ring1, tails = {}, {}, {}
 
     def gather_last(q):
         arrive(mid0[q])
         part0 = x_part(q, 0)
-        last0[q] = [(d, send(part0, part0, shift("x", d))) for d in (2, 1, 3)]
+        if q in DIRECT:
+            last0[q] = [(d, send(part0, part0, shift("x", d))) for d in (2, 1, 3)]
+        else:
+            ring0[q] = [send(part0, part0, right), send(part0, part0, left)]
         arrive(mid1[q])
         part1 = y_part(q, 0)
-        last1[q] = [(d, send(part1, part1, shift("y", d))) for d in (2, 1, 3)]
-        if q == NQ - 1:
+        if q in DIRECT:
+            last1[q] = [(d, send(part1, part1, shift("y", d))) for d in (2, 1, 3)]
             core_send(part0)
             core_send(part1)
+        else:
+            ring1[q] = [send(part1, part1, up), send(part1, part1, down)]
+
+    def gather_on(q):
+        def pass_on(copy, part, peer):
+            copy.wait_recv()
+            return send(part, part, peer)
+
+        tails[q] = [
+            pass_on(ring0[q][0], x_part(q, 3, pl.ds(0, 1)), right),
+            pass_on(ring0[q][1], x_part(q, 1, pl.ds(1, 1)), left),
+            pass_on(ring1[q][0], y_part(q, 3, pl.ds(2, 1)), up),
+            pass_on(ring1[q][1], y_part(q, 1, pl.ds(3, 1)), down),
+        ]
 
     def gather_core(q):
-        if q < NQ - 1:
-            arrive([copy for _, copy in last0[q] + last1[q]])
+        if q not in DIRECT:
+            arrive(tails[q])
             core_send(cc.at[:, :, c, :, columns_of(q)])
             return
         for i in (1, 2, 0):
@@ -242,6 +266,73 @@
             copy.wait_recv()
             core_send(y_part(q, 4 - d))
 
+    def share_weight(q):
+        w_copies[q] = []
+        for i, (d, half) in enumerate(((3, pl.ds(0, 32)), (1, pl.ds(32, 32)))):
+            w_near[q][i].wait_recv()
+            part = weight.at[q, lax.rem(zh + d, 4), half]
+            w_copies[q].append(send(part, part, shift("zh", 4 - d)))
+
+    zh_two, zh_direct, zh_fwd, zx_copies = [], [], [], []
+    ahead, behind = shift("zh", 1), shift("zh", 3)
+
+    def block(part, d):
+        return grad.at[part, c, FIRST_Z, lax.rem(zh + d, 4)]
+
+    def share_zh_two():
+        zh_two.append(send(block(lo, 2), zh_two_in.at[0], behind))
+        zh_two.append(send(block(hi, 2), zh_two_in.at[1], ahead))
+
+    def share_zh_direct():
+        zh_direct.append(send(block(lo, 1), zh_direct_in.at[0], ahead))
+        zh_direct.append(send(block(hi, 3), zh_direct_in.at[1], behind))
+
+    def forward_zh():
+        for half, d, peer in ((0, 3, behind), (1, 1, ahead)):
+            zh_two[half].wait_recv()
+            there = lax.rem(zh + d, 4)
+            for j in range(2):
+                own = grad[2 * half + j, c, FIRST_Z, there]
+                grad[2 * half + j, c, FIRST_Z, there] = own + zh_two_in[half, j]
+            part = block((lo, hi)[half], d)
+            zh_fwd.append(send(part, zh_fwd_in.at[half], peer))
+
+    def sum_zh():
+        arrive(zh_direct + zh_fwd)
+        for j in range(4):
+            half, place = j // 2, j % 2
+            total = grad[j, c, FIRST_Z, zh].astype(F32) + zh_direct_in[half, place].astype(F32)
+            zh_sum[j] = (total + zh_fwd_in[half, place].astype(F32)).astype(BF16)
+            if j < 3:
+                zx_copies.append(send(zh_sum.at[j], zx_in.at[j], shift("x", STEPS[j])))
+
+    def sum_zx():
+        arrive(zx_copies)
+        total = zh_sum[3].astype(F32)
+        for j in range(3):
+            total = total + zx_in[j].astype(F32)
+        total = (total * own_factor[...]).astype(BF16)
+        for t in range(4):
+            for s in range(2):
+                rep_own[t, s] = total[t * 16 : t * 16 + 16, s * 128 : s * 128 + 128]
+        z_copies[FIRST_Z] = []
+        for dy, dz in ((2, 1), (1, 1), (3, 1), (2, 0), (1, 0), (3, 0), (0, 1)):
+            peer = {**shift("y", dy), **shift("zl", dz)}
+            part = rep_own.at[lax.rem(y + dy, 4), lax.rem(zl + dz, 2)]
+            z_copies[FIRST_Z].append(send(part, z_in.at[FIRST_Z, 2 * dy + dz - 1], peer))
+        z_own[FIRST_Z, z] = rep_own[y, zl]
+
+    held = {}
+
+    def base_pair():
+        arrive(held["base_y"])
+        base_sum[...] = base[y] + base_in[0] + base_in[1] + base_in[2]
+        held["base"] = send(base_sum.at[1 - zl], base_far, pair)
+
+    def base_total():
+        held["base"].wait_recv()
+        base_sum[zl] = base_sum[zl] + base_far[...]
+
     def make(*pairs):
         for j, p in pairs:
             product(j, p)
@@ -250,25 +341,21 @@
     product(0, 0)
     pl.semaphore_wait(barrier, len(peers))
     core_share(0, 0)
+    moment_load.wait()
+    factor = (inner_rate / (8 * 32768)) / (jnp.sqrt(moment[0]) + epsilon)
+    for q in RING:
+        weight[q, zh] = factor[:, q * COLS : q * COLS + COLS].astype(BF16)
+    own_factor[...] = factor[:, FIRST_Z * COLS : FIRST_Z * COLS + COLS]
+    w_near, w_copies = {}, {}
+    for q in RING:
+        part = weight.at[q, zh]
+        w_near[q] = [send(part, part, shift("zh", d)) for d in (1, 3)]
     make((1, 0))
     chip_sum(0, 0)
     send_two(0)
-    chip_sum(0, 1)
-    send_two(1)
     make((2, 0))
     chip_sum(1, 0)
     send_right(0)
-    moment_load.wait()
-    factor = (inner_rate / (8 * 32768)) / (jnp.sqrt(moment[0]) + epsilon)
-    w_copies = {}
-
-    def share_weight(q):
-        part = weight.at[q, zh]
-        w_copies[q] = [send(part, part, shift("zh", d)) for d in (2, 1, 3)]
-
-    for q in range(NQ):
-        weight[q, zh] = factor[:, q * COLS : q * COLS + COLS].astype(BF16)
-    share_weight(0)
     for copy in base_loads:
         copy.wait()
     for t in range(4):
@@ -276,54 +363,47 @@
             for q in range(NQ):
                 cols = slice(q * COLS + s * 128, q * COLS + s * 128 + 128)
                 part = slice(t * 16, t * 16 + 16)
-                base[s, t, :, q * 128 : q * 128 + 128] = outer[part, cols] - inner[0, part, cols]
-    base_copy = send(base.at[1 - zl], base_in, pair)
-    for q in range(1, NQ):
-        share_weight(q)
+                base[t, s, :, q * 128 : q * 128 + 128] = outer[part, cols] - inner[0, part, cols]
+    held["base_y"] = [
+        send(base.at[lax.rem(y + d, 4)], base_in.at[d - 1], shift("y", d)) for d in (2, 1, 3)
+    ]
     chip_sum(2, 0)
     send_left(0)
-    make((3, 0), (0, 1))
-    for j in (1, 2, 3):
-        chip_sum(j, 1)
-    chip_sum(3, 0)
-    forward(0)
+    make((0, 1), (1, 1))
     chip_sum(0, 2)
     send_two(2)
-    send_right(1)
-    send_left(1)
-    make((1, 1))
-    forward(1)
+    make((3, 0))
+    forward(0)
+    share_weight(0)
+    make((2, 1))
+    for j in range(4):
+        chip_sum(j, 1)
+    share_zh_two()
     chip_sum(0, 3)
     send_two(3)
-    make((2, 1))
     chip_sum(1, 2)
     send_right(2)
-    make((3, 1))
+    share_weight(2)
+    share_weight(3)
+    share_zh_direct()
+    base_pair()
     chip_sum(2, 2)
     send_left(2)
-    for j, q in ((3, 2), (1, 3), (2, 3), (3, 3)):
-        chip_sum(j, q)
+    make((3, 1))
+    forward(2)
+    chip_sum(1, 3)
+    send_right(3)
+    chip_sum(2, 3)
+    send_left(3)
+    chip_sum(3, 0)
     mom_load.wait()
 
-    held = {}
-
-    def base_pair():
-        base_copy.wait_recv()
-        for t in range(4):
-            base_sum[t] = base[zl, t] + base_in[t]
-        held["base"] = [
-            send(base_sum.at[lax.rem(y + d, 4)], base_y.at[d - 1], shift("y", d)) for d in (2, 1, 3)
-        ]
-
-    def base_total():
-        arrive(held["base"])
-        base_y[3] = base_sum[y] + base_y[0] + base_y[1] + base_y[2]
+    def ready_sums():
+        chip_sum(3, 2)
+        chip_sum(3, 3)
 
     def fwd_and_next(q):
         forward(q)
-        if q == 2:
-            send_right(3)
-            send_left(3)
 
     def nm_pair():
         part = nm.at[y, zl]
@@ -334,15 +414,13 @@
         part = nm.at[y]
         held["nm_y"] = [send(part, part, shift("y", d)) for d in (2, 1, 3)]
 
-    done = (7.6, 11.8, 16.0, 19.0)
-    events = [(9.0, fwd_and_next, (2,)), (13.2, fwd_and_next, (3,))]
-    events += [(11.3, base_pair, ()), (15.5, base_total, ())]
-    stages = (finish_x, finish_y, finish_z, gather_mid, gather_last, gather_core)
-    for q in range(NQ):
-        waits = (0, 3.5, 8, 12.5, 16, 22) if q < NQ - 1 else (0, 3, 6.8, 10.5, 13.5, 18.5)
-        events += [(done[q] + wait, stage, (q,)) for wait, stage in zip(waits, stages)]
-    events += [(done[-1] + 7.1, nm_pair, ()), (done[-1] + 11.1, nm_y, ())]
-    for _, stage, operands in sorted(events, key=lambda event: event[0]):
+    stages = {
+        "X": finish_x, "F": fwd_and_next, "Y": finish_y, "Z": finish_z, "M": gather_mid,
+        "L": gather_last, "G": gather_on, "C": gather_core,
+    }
+    extra = {"cs": ready_sums, "zf": forward_zh, "zs": sum_zh, "zx": sum_zx, "bt": base_total, "np": nm_pair, "ny": nm_y}
+    for name in ORDER:
+        stage, operands = (extra[name], ()) if name in extra else (stages[name[0]], (int(name[1]),))
         stage(*operands)
     arrive(held["nm_y"])
     arrive(shared)
@@ -352,19 +430,20 @@
 
 def write(nm, cc, new_p, new_m, out, buf_p, buf_m, sem):
     zh, x, c = (lax.axis_index(a) for a in SHARD)
-    copies = [pltpu.make_async_copy(cc, out, sem.at[0])]
-    copies[0].start()
+    copies = [pltpu.make_async_copy(cc.at[h], out.at[h], sem.at[h]) for h in range(4)]
+    for copy in copies:
+        copy.start()
     buf_p[...] = cc[zh, x, c].astype(F32)
-    copies.append(pltpu.make_async_copy(buf_p, new_p, sem.at[1]))
-    copies[1].start()
+    copies.append(pltpu.make_async_copy(buf_p, new_p, sem.at[4]))
+    copies[4].start()
     for t in range(4):
         for s in range(2):
             for q in range(NQ):
                 cols = slice(q * COLS + s * 128, q * COLS + s * 128 + 128)
                 value = nm[t, s, :, q * 128 : q * 128 + 128].astype(F32)
                 buf_m[t * 16 : t * 16 + 16, cols] = value
-    copies.append(pltpu.make_async_copy(buf_m, new_m, sem.at[2]))
-    copies[2].start()
+    copies.append(pltpu.make_async_copy(buf_m, new_m, sem.at[5]))
+    copies[5].start()
     for copy in copies:
         copy.wait()
 
@@ -395,10 +474,17 @@
             pltpu.VMEM((1, 64, 1024), F32),
             pltpu.VMEM((64, 1024), F32),
             pltpu.VMEM((64, 1024), F32),
-            pltpu.VMEM((2, 4, 16, NQ * 128), F32),
-            pltpu.VMEM((4, 16, NQ * 128), F32),
-            pltpu.VMEM((4, 16, NQ * 128), F32),
-            pltpu.VMEM((4, 16, NQ * 128), F32),
+            pltpu.VMEM((4, 2, 16, NQ * 128), F32),
+            pltpu.VMEM((3, 2, 16, NQ * 128), F32),
+            pltpu.VMEM((2, 16, NQ * 128), F32),
+            pltpu.VMEM((16, NQ * 128), F32),
+            pltpu.VMEM((64, COLS), F32),
+            pltpu.VMEM((2, 2, 64, COLS), BF16),
+            pltpu.VMEM((2, 2, 64, COLS), BF16),
+            pltpu.VMEM((2, 2, 64, COLS), BF16),
+            pltpu.VMEM((4, 64, COLS), BF16),
+            pltpu.VMEM((3, 64, COLS), BF16),
+            pltpu.VMEM((4, 2, 16, 128), BF16),
             pltpu.SemaphoreType.DMA((32,)),
             pltpu.SemaphoreType.DMA((SEMS,)),
             pltpu.SemaphoreType.DMA((SEMS,)),
@@ -419,7 +505,7 @@
         scratch_shapes=[
             pltpu.VMEM((64, 1024), F32),
             pltpu.VMEM((64, 1024), F32),
-            pltpu.SemaphoreType.DMA((3,)),
+            pltpu.SemaphoreType.DMA((6,)),
         ],
         compiler_params=pltpu.CompilerParams(vmem_limit_bytes=8 * 2**20),
     )(nm, cc)

time: 68.8 us -> 62.1 us (0.903)
  Pallas kernels: 68.1 us -> 61.4 us
    pallas_call x1, Pallas kernels: 65.9 us -> 59.2 us  [per_device(): pl.pallas_call(kernel, out_shape=(pltpu.VMEM((4, 2, 16, NQ * 128), BF16),...]
where the time goes in v3:
time: 62.1 us; the launch traced here: 62 us
  Pallas kernels  61.4 us (99%)
  between operations  0.64 us (1%)
    pallas_call x1, Pallas kernels, per_device(): pl.pallas_call(kernel, out_shape=(pltpu.VMEM((4, 2, 16, NQ * 128), BF16),...  59.2 us
    pallas_call x1, Pallas kernels, per_device(): pl.pallas_call(write, out_shape=(jax.ShapeDtypeStruct((64, 1024), F32), j...  2.22 us

profile of v3, /device:TPU:1, one launch (start us, length us, event | category | flops | bytes accessed | tf_op | source)
XLA Modules:
  0.0 62.0 jit_solution(5020602299011326843)
XLA Ops:
  0.6 59.2 %shard_map.85 = (bf16[4,2,16,512]{3,2,1,0:T(8,128)(2,1)S(1)}, bf16[4,4,2,64,1024]{4,3,2,1,0:T(8,128)(2,1)S(1)}) custom-call(bf16[1024,2048]{1,0:T(8,128)(2,1)} %act.1, bf16[1024,1024]{1,0:T(8,128)(2,1)} %cot.1, f32[1,64,1024]{2,1,0:T(8,128)} %inner_h.1, f32[1,64,1024]{2,1,0:T(8,128)} %moment_h.1, f32[64,1024]{1,0:T(8,128)} %outer_h.1, f32[64,1024]{1,0:T(8,128)} %mom_h.1), custom_call_target="tpu_custom_call" | custom-call | tf_op jit(solution)/shard_map/pallas_call | solution.py:455
  59.8 2.2 %shard_map.86 = (f32[64,1024]{1,0:T(8,128)}, f32[64,1024]{1,0:T(8,128)}, bf16[4,4,2,64,1024]{4,3,2,1,0:T(8,128)(2,1)}) custom-call(bf16[4,2,16,512]{3,2,1,0:T(8,128)(2,1)S(1)} %get-tuple-element.8.nm, bf16[4,4,2,64,1024]{4,3,2,1,0:T(8,128)(2,1)S(1)} %get-tuple-element.9.cc), custom_call_target="tpu_custom_call" | custom-call | tf_op jit(solution)/shard_map/pallas_call | solution.py:496

commit v4 on v3

--- a/solution.py
+++ b/solution.py
@@ -24,7 +24,7 @@
 COLS = 1024 // NQ
 RING = (0, 2, 3)
 FIRST_Z = 1
-ORDER = ("X0", "F3", "Y0", "cs", "zf", "X2", "X3", "Y2", "bt", "Z0", "Y3", "zs", "Z2", "M0", "zx", "Z3", "M2", "L0", "Z1", "np", "M3", "L2", "G0", "M1", "ny", "L3", "G2", "L1", "C0", "C2", "C3", "C1")
+ORDER = ("X0", "F3", "Y0", "cs", "zf", "X2", "X3", "Y2", "bt", "Z0", "Y3", "zs", "Z2", "M0", "zx", "Z3", "M2", "L0", "Z1", "np", "M3", "L2", "M1", "ny", "G0", "L3", "G2", "L1", "C0", "C3", "C2", "C1")
 DIRECT = (1, 3)
 SEMS = 200
 STEPS = (2, 1, 3, 0)
@@ -124,8 +124,8 @@
                     part = value[row : row + 64, q * COLS : q * COLS + COLS]
                     grad[j, k, 2 * p + q, h] = part
 
-    def core_share(j, p):
-        for q in (2 * p, 2 * p + 1):
+    def core_share(j, p, places=(0, 1)):
+        for q in (2 * p + place for place in places):
             core_copies[j, q] = send(grad.at[j, 1 - c, q], core_in.at[j, q], core)
 
     def chip_sum(j, q):
@@ -340,7 +340,7 @@
 
     product(0, 0)
     pl.semaphore_wait(barrier, len(peers))
-    core_share(0, 0)
+    core_share(0, 0, (0,))
     moment_load.wait()
     factor = (inner_rate / (8 * 32768)) / (jnp.sqrt(moment[0]) + epsilon)
     for q in RING:
@@ -353,6 +353,7 @@
     make((1, 0))
     chip_sum(0, 0)
     send_two(0)
+    core_share(0, 0, (1,))
     make((2, 0))
     chip_sum(1, 0)
     send_right(0)

time: 62.1 us -> 61.9 us (level)
  no operation moved by 1% of the time
where the time goes in v4:
time: 61.9 us; the launch traced here: 61.8 us
  Pallas kernels  61.2 us (99%)
  between operations  0.64 us (1%)
    pallas_call x1, Pallas kernels, per_device(): pl.pallas_call(kernel, out_shape=(pltpu.VMEM((4, 2, 16, NQ * 128), BF16),...  59 us
    pallas_call x1, Pallas kernels, per_device(): pl.pallas_call(write, out_shape=(jax.ShapeDtypeStruct((64, 1024), F32), j...  2.22 us

profile of v4, /device:TPU:1, one launch (start us, length us, event | category | flops | bytes accessed | tf_op | source)
XLA Modules:
  0.0 61.8 jit_solution(16280488792027464353)
XLA Ops:
  0.6 59.0 %shard_map.85 = (bf16[4,2,16,512]{3,2,1,0:T(8,128)(2,1)S(1)}, bf16[4,4,2,64,1024]{4,3,2,1,0:T(8,128)(2,1)S(1)}) custom-call(bf16[1024,2048]{1,0:T(8,128)(2,1)} %act.1, bf16[1024,1024]{1,0:T(8,128)(2,1)} %cot.1, f32[1,64,1024]{2,1,0:T(8,128)} %inner_h.1, f32[1,64,1024]{2,1,0:T(8,128)} %moment_h.1, f32[64,1024]{1,0:T(8,128)} %outer_h.1, f32[64,1024]{1,0:T(8,128)} %mom_h.1), custom_call_target="tpu_custom_call" | custom-call | tf_op jit(solution)/shard_map/pallas_call | solution.py:456
  59.6 2.2 %shard_map.86 = (f32[64,1024]{1,0:T(8,128)}, f32[64,1024]{1,0:T(8,128)}, bf16[4,4,2,64,1024]{4,3,2,1,0:T(8,128)(2,1)}) custom-call(bf16[4,2,16,512]{3,2,1,0:T(8,128)(2,1)S(1)} %get-tuple-element.8.nm, bf16[4,4,2,64,1024]{4,3,2,1,0:T(8,128)(2,1)S(1)} %get-tuple-element.9.cc), custom_call_target="tpu_custom_call" | custom-call | tf_op jit(solution)/shard_map/pallas_call | solution.py:497

commit v5 on v4

--- a/solution.py
+++ b/solution.py
@@ -347,13 +347,18 @@
         weight[q, zh] = factor[:, q * COLS : q * COLS + COLS].astype(BF16)
     own_factor[...] = factor[:, FIRST_Z * COLS : FIRST_Z * COLS + COLS]
     w_near, w_copies = {}, {}
-    for q in RING:
+
+    def start_weight(q):
         part = weight.at[q, zh]
         w_near[q] = [send(part, part, shift("zh", d)) for d in (1, 3)]
+
+    start_weight(0)
     make((1, 0))
     chip_sum(0, 0)
     send_two(0)
     core_share(0, 0, (1,))
+    for q in (2, 3):
+        start_weight(q)
     make((2, 0))
     chip_sum(1, 0)
     send_right(0)

time: 61.9 us -> 61.9 us (level)
  no operation moved by 1% of the time
where the time goes in v5:
time: 61.9 us
  Pallas kernels  61.2 us (99%)
  between operations  0.64 us (1%)
    pallas_call x1, Pallas kernels, per_device(): pl.pallas_call(kernel, out_shape=(pltpu.VMEM((4, 2, 16, NQ * 128), BF16),...  59 us
    pallas_call x1, Pallas kernels, per_device(): pl.pallas_call(write, out_shape=(jax.ShapeDtypeStruct((64, 1024), F32), j...  2.22 us

profile of v5, /device:TPU:1, one launch (start us, length us, event | category | flops | bytes accessed | tf_op | source)
XLA Modules:
  0.0 61.9 jit_solution(11962978586632799662)
XLA Ops:
  0.6 59.0 %shard_map.85 = (bf16[4,2,16,512]{3,2,1,0:T(8,128)(2,1)S(1)}, bf16[4,4,2,64,1024]{4,3,2,1,0:T(8,128)(2,1)S(1)}) custom-call(bf16[1024,2048]{1,0:T(8,128)(2,1)} %act.1, bf16[1024,1024]{1,0:T(8,128)(2,1)} %cot.1, f32[1,64,1024]{2,1,0:T(8,128)} %inner_h.1, f32[1,64,1024]{2,1,0:T(8,128)} %moment_h.1, f32[64,1024]{1,0:T(8,128)} %outer_h.1, f32[64,1024]{1,0:T(8,128)} %mom_h.1), custom_call_target="tpu_custom_call" | custom-call | tf_op jit(solution)/shard_map/pallas_call | solution.py:461
  59.6 2.2 %shard_map.86 = (f32[64,1024]{1,0:T(8,128)}, f32[64,1024]{1,0:T(8,128)}, bf16[4,4,2,64,1024]{4,3,2,1,0:T(8,128)(2,1)}) custom-call(bf16[4,2,16,512]{3,2,1,0:T(8,128)(2,1)S(1)} %get-tuple-element.8.nm, bf16[4,4,2,64,1024]{4,3,2,1,0:T(8,128)(2,1)S(1)} %get-tuple-element.9.cc), custom_call_target="tpu_custom_call" | custom-call | tf_op jit(solution)/shard_map/pallas_call | solution.py:502
